TPU v7x, 256 devices: a whole 4x4x8 slice. The times are simulated.
256 devices in a mesh: dp: 8 (over z), expert: 32 (over y, x, core).
Axes of the slice: x: 4, y: 4, z: 8, core: 2. Of those that a mesh axis runs over, the one named last changes fastest.
Arguments:
- tokens: bfloat16 [1024, 7168], P(('dp', 'expert')), may hold values from -6 to 6
- routes: int32 [1024, 8], P(('dp', 'expert')), may hold values from 0 to 31, all different within a row; in each aligned block of 4 rows (0 to 3, 4 to 7, ...) at most 2 rows name the same one
- gate_scores: float32 [1024, 8], P(('dp', 'expert')), may hold values from 0.1 to 1
- w_gate: bfloat16 [32, 7168, 2048], P('expert', None, 'dp'), may hold values from -0.0625 to 0.0625
- w_up: bfloat16 [32, 7168, 2048], P('expert', None, 'dp'), may hold values from -0.0625 to 0.0625
- w_down: bfloat16 [32, 2048, 7168], P('expert', 'dp'), may hold values from -0.125 to 0.125
Outputs:
- mixed_out: bfloat16 [1024, 7168], P(('dp', 'expert'))
Inputs may be any that keep to these rules, and one draw needn't show every extreme that they name: `routes`: each row names 8 different experts. In the rows of one device (aligned blocks of 4 rows) no expert is named by more than 2 rows, a bound that some block reaches.
All inputs are finite; a program needn't handle non-finite values.
Results may differ from a plain program's by a relative error of at most 0.0098.
Values may be sent and summed in bfloat16 or wider, within the bound.
No kernel may reach another device: no remote copies, remote signals or barrier semaphores. Data moves between devices by JAX's collectives and lax.ppermute only.
A program may use at most 128 MiB of HBM per device.

v0:
```python
import jax
import jax.numpy as jnp
from jax import lax
from jax.sharding import PartitionSpec as P


def slots_of(route_ids, owners):
    matched = (route_ids[:, None] == jnp.arange(owners, dtype=jnp.int32)[None, :]).astype(jnp.int32)
    before = jnp.cumsum(matched, axis=0) - matched
    return jnp.sum(before * matched, axis=1)


def expert_rows(picked_rows, gate_mat, up_mat, down_mat):
    gate_act = jnp.dot(picked_rows, gate_mat, preferred_element_type=jnp.float32)
    up_act = jnp.dot(picked_rows, up_mat, preferred_element_type=jnp.float32)
    hidden = (jax.nn.silu(gate_act) * up_act).astype(jnp.bfloat16)
    return jnp.dot(hidden, down_mat, preferred_element_type=jnp.float32)


def shards(tokens, routes, gate_scores, w_gate, w_up, w_down):
    tok_rows, model_width = tokens.shape
    route_count = routes.shape[1]
    owners = lax.axis_size("expert")
    capacity = tok_rows // 4 + 1
    gate_mat, up_mat, down_mat = (w_gate[0], w_up[0], w_down[0])
    source = jnp.repeat(jnp.arange(tok_rows, dtype=jnp.int32), route_count)
    flat_ids = routes.reshape(-1)
    own_slots = slots_of(flat_ids, owners)
    target_row = flat_ids * capacity + own_slots
    outgoing = (
        jnp.zeros((owners * capacity, model_width), jnp.bfloat16).at[target_row].set(tokens[source])
    )
    arrived = lax.all_to_all(
        outgoing.reshape(owners, capacity, model_width),
        "expert",
        split_axis=0,
        concat_axis=0,
        tiled=True,
    )
    blocks = lax.all_gather(arrived[None], "dp", axis=0, tiled=True)
    block_shape = blocks.shape[:-1] + (model_width,)
    flat_out = expert_rows(blocks.reshape(-1, model_width), gate_mat, up_mat, down_mat)
    partial_value = flat_out.reshape(block_shape)
    summed = lax.psum_scatter(
        partial_value.astype(jnp.bfloat16), "dp", scatter_dimension=0, tiled=True
    ).astype(jnp.float32)[0]
    returned = lax.all_to_all(
        summed.astype(jnp.bfloat16), "expert", split_axis=0, concat_axis=0, tiled=True
    ).astype(summed.dtype)
    lookup = flat_ids * capacity + own_slots
    picked = returned.reshape(owners * capacity, model_width)[lookup]
    mixed_out = jnp.sum(
        picked.reshape(tok_rows, route_count, model_width) * gate_scores[..., None], axis=1
    )
    return mixed_out.astype(jnp.bfloat16)


def solution(mesh):
    return jax.shard_map(
        shards,
        mesh=mesh,
        in_specs=(
            P(("dp", "expert"), None),
            P(("dp", "expert"), None),
            P(("dp", "expert"), None),
            P("expert", None, "dp"),
            P("expert", None, "dp"),
            P("expert", "dp", None),
        ),
        out_specs=P(("dp", "expert"), None),
        check_vma=False,
    )
```

profile of v0, /device:TPU:1, one launch (start us, length us, event | category | flops | bytes accessed | tf_op | source)
XLA Modules:
  0.0 270.3 jit_solution(8164090373457561248)
XLA Ops:
  6.5 0.0 copy-start
  6.5 0.0 all-gather.3.cloned.1.call-start
  6.5 0.8 eq.15
  7.3 0.7 broadcast_multiply_fusion
  8.0 0.1 fusion.16
  8.1 0.1 reduce_window_sum.11
  8.1 0.2 select_reduce_fusion
  8.3 0.1 mul.33
  8.4 0.1 reshape.80
  8.5 0.0 copy-done
  8.5 2.8 %scatter_custom_fusion = bf16[64,7168]{1,0:T(8,128)(2,1)S(1)} fusion(s32[32]{0:T(128)S(1)} %fusion.17, bf16[4,7168]{1,0:T(4,128)(2,1)S(1)} %copy-done, s32[1024]{0:T(1024)S(1)} %pad_clamp_fusion.1, bf16[]{:T(256)} %constant.7.clone.1), kind=kCustom, calls=%fused_computation.13 | custom fusion | bytes 917506 | tf_op jit(solution)/shard_map/scatter | solution.py:31
  11.4 0.3 reshape.81
  11.7 24.1 %all_to_all.10 = bf16[32,2,7168]{2,1,0:T(2,128)(2,1)} all-to-all(bf16[32,2,7168]{2,1,0:T(2,128)(2,1)S(1)} %reshape.81), channel_id=1, replica_groups=mesh['dp'=8,'expert'=32] {'expert'}, dimensions={0} | all-to-all | bytes 1835008 | tf_op jit(solution)/shard_map/all_to_all | solution.py:33
  35.8 0.0 all-gather.3.cloned.1.call-update
  35.9 0.2 reduce-scatter.2.cloned.1.call-start
  36.1 83.1 %all-gather.3.cloned.1.call-done = bf16[256,2,7168]{2,1,0:T(2,128)(2,1)} async-done(((bf16[32,2,7168]{2,1,0:T(2,128)(2,1)}), bf16[256,2,7168]{2,1,0:T(2,128)(2,1)}) %all-gather.3.cloned.1.call-update) | async-done | bytes 7340048 | tf_op jit(solution)/shard_map/all_gather | solution.py:40
  119.2 15.4 %reshape.82 = bf16[512,7168]{1,0:T(8,128)(2,1)} reshape(bf16[256,2,7168]{2,1,0:T(2,128)(2,1)} %all-gather.3.cloned.1.call-done) | data formatting | bytes 14680064 | tf_op jit(solution)/shard_map/reshape | solution.py:42
  134.6 6.3 %fusion.3 = f32[512,256]{1,0:T(8,128)S(1)} fusion(bf16[512,7168]{1,0:T(8,128)(2,1)} %reshape.82, bf16[1,7168,256]{2,1,0:T(8,128)(2,1)} %param.9), kind=kOutput, calls=%fused_computation.7 | convolution fusion | flops 1879048192 | bytes 11534336 | tf_op jit(solution)/shard_map/dot_general | solution.py:14
  140.9 0.0 copy-done.1
  141.0 0.9 copy-done.3
  141.9 2.1 fusion.8
  143.9 0.1 dot_general.13
  144.0 7.1 %convolution_convert_fusion = bf16[8,32,2,7168]{3,1,2,0:T(8,128)(2,1)} fusion(bf16[1,256,7168]{2,1,0:T(8,128)(2,1)} %param.11, bf16[8,32,2,256]{3,2,1,0:T(2,128)(2,1)S(1)} %dot_general.13), kind=kOutput, calls=%fused_computation.3 | convolution fusion | flops 1882718208 | bytes 11272192 | tf_op jit(solution)/shard_map/dot_general | solution.py:17
  151.1 0.0 reduce-scatter.2.cloned.1.call-update
  151.2 83.9 %reduce-scatter.2.cloned.1.call-done = bf16[1,32,2,7168]{3,1,2,0:T(8,128)(2,1)} async-done(((bf16[8,32,2,7168]{3,1,2,0:T(8,128)(2,1)}), bf16[1,32,2,7168]{3,1,2,0:T(8,128)(2,1)}) %reduce-scatter.2.cloned.1.call-update) | async-done | bytes 917520 | tf_op jit(solution)/shard_map/reduce_scatter | solution.py:44
  235.1 3.0 %copy.11 = bf16[32,2,7168]{2,1,0:T(2,128)(2,1)} copy(bf16[32,2,7168]{2,0,1:T(8,128)(2,1)} %bitcast.32) | data formatting | bytes 1835008 | tf_op jit(solution)/shard_map/convert_element_type | solution.py:48
  238.1 7.6 %all-to-all-start.1 = ((bf16[32,2,7168]{2,1,0:T(2,128)(2,1)}), bf16[32,2,7168]{2,1,0:T(2,128)(2,1)S(1)}, u32[]{:S(2)}, u32[]{:S(2)}) async-start(bf16[32,2,7168]{2,1,0:T(2,128)(2,1)} %copy.11), calls=%async_computation.2 | async-start | bytes 1835008 | tf_op jit(solution)/shard_map/all_to_all | solution.py:47
  245.7 15.6 %all-to-all-done.1 = bf16[32,2,7168]{2,1,0:T(2,128)(2,1)S(1)} async-done(((bf16[32,2,7168]{2,1,0:T(2,128)(2,1)}), bf16[32,2,7168]{2,1,0:T(2,128)(2,1)S(1)}, u32[]{:S(2)}, u32[]{:S(2)}) %all-to-all-start.1) | async-done | bytes 917536 | tf_op jit(solution)/shard_map/all_to_all | solution.py:47
  261.3 0.3 reshape.87
  261.6 0.0 copy-start.2
  261.6 0.9 gather_fusion
  262.5 1.0 fusion.11
  (8 shorter events, 0.0 us)
Async XLA Ops:
  6.5 2.0 copy-start
  6.5 112.6 %all-gather.3.cloned.1.call-start = ((), (), s32[]{:S(2)}) async-start(), calls=%async_computation.4 | async-start | bytes 8257536 | tf_op jit(solution)/shard_map/all_gather | solution.py:40
  35.9 199.2 %reduce-scatter.2.cloned.1.call-start = ((), (), s32[]{:S(2)}) async-start(), calls=%async_computation.3 | async-start | bytes 8257536 | tf_op jit(solution)/shard_map/reduce_scatter | solution.py:44
  134.6 6.3 %copy-start.1 = (bf16[512,7168]{1,0:T(8,128)(2,1)S(1)}, bf16[512,7168]{1,0:T(8,128)(2,1)}, u32[]{:S(2)}) copy-start(bf16[512,7168]{1,0:T(8,128)(2,1)} %reshape.82) | copy-start | bytes 22020100
  134.6 7.3 %copy-start.3 = (bf16[1,7168,256]{2,1,0:T(8,128)(2,1)S(1)}, bf16[1,7168,256]{2,1,0:T(8,128)(2,1)}, u32[]{:S(2)}) copy-start(bf16[1,7168,256]{2,1,0:T(8,128)(2,1)} %param.10) | copy-start | bytes 11010052
  238.1 23.2 %all-to-all-start.1 = ((bf16[32,2,7168]{2,1,0:T(2,128)(2,1)}), bf16[32,2,7168]{2,1,0:T(2,128)(2,1)S(1)}, u32[]{:S(2)}, u32[]{:S(2)}) async-start(bf16[32,2,7168]{2,1,0:T(2,128)(2,1)} %copy.11), calls=%async_computation.2 | async-start | bytes 1835008 | tf_op jit(solution)/shard_map/all_to_all | solution.py:47
  261.6 0.9 copy-start.2
Sparse Core Ops, SparseCore 0:
  36.0 83.1 all-gather.2
  151.3 83.7 reduce-scatter.1
where the time goes:
time: 271 us; the launch traced here: 270 us
  waiting for transfers between devices  183 us (68%)
  local copies, waits for them, and re-layouts  24.7 us (9%)
  blocking collectives  24.1 us (9%)
  matrix products  15.5 us (6%)
  between operations  13.5 us (5%)
  starting transfers between devices  7.81 us (3%)
    reduce_scatter x1, waiting for transfers between devices, shards(): lax.psum_scatter(partial_value.astype(jnp.bfloat16), 'dp', scatter_dimens...  83.9 us
    all_gather x1, waiting for transfers between devices, shards(): blocks = lax.all_gather(arrived[None], 'dp', axis=0, tiled=True)  83.1 us
    all_to_all x1, blocking collectives, shards(): lax.all_to_all(outgoing.reshape(owners, capacity, model_width), 'expert',...  24.1 us
    all_to_all x1, waiting for transfers between devices, shards(): lax.all_to_all(summed.astype(jnp.bfloat16), 'expert', split_axis=0, conca...  15.6 us
    reshape x1, local copies, waits for them, and re-layouts, shards(): blocks.reshape(-1, model_width)  15.4 us
    all_to_all x1, starting transfers between devices, shards(): lax.all_to_all(summed.astype(jnp.bfloat16), 'expert', split_axis=0, conca...  7.59 us
    dot_general x1, matrix products, expert_rows(): return jnp.dot(hidden, down_mat, preferred_element_type=jnp.float32)  7.1 us
    dot_general x1, matrix products, expert_rows(): jnp.dot(picked_rows, gate_mat, preferred_element_type=jnp.float32)  6.33 us
  transfers between devices with their start and end apart: 3, of which 3 were waited for; matrix products, arithmetic and copies ran while one was open for 0% of the time, Pallas kernels for 0%

commit v1 on v0

--- a/solution.py
+++ b/solution.py
@@ -37,7 +37,15 @@
         concat_axis=0,
         tiled=True,
     )
-    blocks = lax.all_gather(arrived[None], "dp", axis=0, tiled=True)
+
+    def _press_windows(my_data, a_name):
+        extent = jax.lax.axis_size(a_name)
+        ledger = [extent if w == 0 else 1 for w in range(my_data.ndim)]
+        return jax.lax.all_to_all(
+            jnp.tile(my_data, ledger), a_name, split_axis=0, concat_axis=0, tiled=True
+        )
+
+    blocks = _press_windows(arrived[None], "dp")
     block_shape = blocks.shape[:-1] + (model_width,)
     flat_out = expert_rows(blocks.reshape(-1, model_width), gate_mat, up_mat, down_mat)
     partial_value = flat_out.reshape(block_shape)

time: 271 us -> 359 us (1.32)
  blocking collectives: 24.1 us -> 195 us
  waiting for transfers between devices: 183 us -> 95 us
  local copies, waits for them, and re-layouts: 24.7 us -> 29.7 us
    all_to_all x0 -> x1, blocking collectives: none -> 171 us  [_press_windows(): jax.lax.all_to_all(jnp.tile(my_data, ledger), a_name, split_axis=0, conca...]
    all_gather x1 -> x0, waiting for transfers between devices: 83.1 us -> none  [shards(): blocks = lax.all_gather(arrived[None], 'dp', axis=0, tiled=True)]
    another operation x0 -> x1, local copies, waits for them, and re-layouts: none -> 4.95 us  [_press_windows(): jnp.tile(my_data, ledger)]
    reduce_scatter x1, waiting for transfers between devices: 83.9 us -> 79.4 us  [shards(): lax.psum_scatter(partial_value.astype(jnp.bfloat16), 'dp', scatter_dimens...]
  transfers between devices with their start and end apart: 3 -> 2, of which waited for: 3 -> 2; matrix products, arithmetic and copies ran while one was open for 0% -> 0% of each run, Pallas kernels for 0% -> 0%
where the time goes in v1:
time: 359 us; the launch traced here: 358 us
  blocking collectives  195 us (54%)
  waiting for transfers between devices  95 us (26%)
  local copies, waits for them, and re-layouts  29.7 us (8%)
  matrix products  15.5 us (4%)
  between operations  13.5 us (4%)
  starting transfers between devices  7.6 us (2%)
    all_to_all x1, blocking collectives, _press_windows(): jax.lax.all_to_all(jnp.tile(my_data, ledger), a_name, split_axis=0, conca...  171 us
    reduce_scatter x1, waiting for transfers between devices, shards(): lax.psum_scatter(partial_value.astype(jnp.bfloat16), 'dp', scatter_dimens...  79.4 us
    all_to_all x1, blocking collectives, shards(): lax.all_to_all(outgoing.reshape(owners, capacity, model_width), 'expert',...  24 us
    all_to_all x1, waiting for transfers between devices, shards(): lax.all_to_all(summed.astype(jnp.bfloat16), 'expert', split_axis=0, conca...  15.6 us
    reshape x1, local copies, waits for them, and re-layouts, shards(): blocks.reshape(-1, model_width)  15.4 us
    all_to_all x1, starting transfers between devices, shards(): lax.all_to_all(summed.astype(jnp.bfloat16), 'expert', split_axis=0, conca...  7.59 us
  transfers between devices with their start and end apart: 2, of which 2 were waited for; matrix products, arithmetic and copies ran while one was open for 0% of the time, Pallas kernels for 0%

profile of v1, /device:TPU:1, one launch (start us, length us, event | category | flops | bytes accessed | tf_op | source)
XLA Modules:
  0.0 358.0 jit_solution(7936554085524825750)
XLA Ops:
  6.5 0.0 copy-start
  6.5 0.0 reduce-scatter.2.cloned.1.call-start
  6.5 0.8 eq.15
  7.3 0.7 broadcast_multiply_fusion
  8.0 0.1 fusion.16
  8.1 0.1 reduce_window_sum.11
  8.1 0.2 select_reduce_fusion
  8.3 0.1 mul.33
  8.4 0.1 reshape.83
  8.5 0.0 copy-done
  8.5 2.8 scatter_custom_fusion
  11.4 0.3 reshape.84
  11.7 24.0 %all_to_all.15 = bf16[32,2,7168]{2,1,0:T(2,128)(2,1)S(1)} all-to-all(bf16[32,2,7168]{2,1,0:T(2,128)(2,1)S(1)} %reshape.84), channel_id=1, replica_groups=mesh['dp'=8,'expert'=32] {'expert'}, dimensions={0} | all-to-all | bytes 1835008 | tf_op jit(solution)/shard_map/all_to_all | solution.py:33
  35.7 4.9 %tile.2 = bf16[8,32,2,7168]{3,2,1,0:T(2,128)(2,1)S(1)} broadcast(bf16[32,2,7168]{2,1,0:T(2,128)(2,1)S(1)} %all_to_all.15), dimensions={1,2,3} | broadcast | bytes 8257536 | tf_op jit(solution)/shard_map/tile | solution.py:45
  40.7 170.6 %all_to_all.16 = bf16[8,32,2,7168]{3,2,1,0:T(2,128)(2,1)} all-to-all(bf16[8,32,2,7168]{3,2,1,0:T(2,128)(2,1)S(1)} %tile.2), channel_id=1, replica_groups=mesh['dp'=8,'expert'=32] {'dp'}, dimensions={0} | all-to-all | bytes 14680064 | tf_op jit(solution)/shard_map/all_to_all | solution.py:44
  211.3 15.4 %reshape.85 = bf16[512,7168]{1,0:T(8,128)(2,1)} reshape(bf16[8,32,2,7168]{3,2,1,0:T(2,128)(2,1)} %all_to_all.16) | data formatting | bytes 14680064 | tf_op jit(solution)/shard_map/reshape | solution.py:50
  226.8 6.3 %fusion.3 = f32[512,256]{1,0:T(8,128)S(1)} fusion(bf16[512,7168]{1,0:T(8,128)(2,1)} %reshape.85, bf16[1,7168,256]{2,1,0:T(8,128)(2,1)} %param.9), kind=kOutput, calls=%fused_computation.7 | convolution fusion | flops 1879048192 | bytes 11534336 | tf_op jit(solution)/shard_map/dot_general | solution.py:14
  233.1 0.0 copy-done.1
  233.1 0.9 copy-done.3
  234.0 2.1 fusion.8
  236.1 0.1 dot_general.13
  236.2 7.1 %convolution_convert_fusion = bf16[8,32,2,7168]{3,1,2,0:T(8,128)(2,1)} fusion(bf16[1,256,7168]{2,1,0:T(8,128)(2,1)} %param.11, bf16[8,32,2,256]{3,2,1,0:T(2,128)(2,1)S(1)} %dot_general.13), kind=kOutput, calls=%fused_computation.3 | convolution fusion | flops 1882718208 | bytes 11272192 | tf_op jit(solution)/shard_map/dot_general | solution.py:17
  243.3 0.0 reduce-scatter.2.cloned.1.call-update
  243.3 79.4 %reduce-scatter.2.cloned.1.call-done = bf16[1,32,2,7168]{3,1,2,0:T(8,128)(2,1)} async-done(((bf16[8,32,2,7168]{3,1,2,0:T(8,128)(2,1)}), bf16[1,32,2,7168]{3,1,2,0:T(8,128)(2,1)}) %reduce-scatter.2.cloned.1.call-update) | async-done | bytes 917520 | tf_op jit(solution)/shard_map/reduce_scatter | solution.py:52
  322.7 3.0 copy.11
  325.7 7.6 %all-to-all-start.2 = ((bf16[32,2,7168]{2,1,0:T(2,128)(2,1)}), bf16[32,2,7168]{2,1,0:T(2,128)(2,1)S(1)}, u32[]{:S(2)}, u32[]{:S(2)}) async-start(bf16[32,2,7168]{2,1,0:T(2,128)(2,1)} %copy.11), calls=%async_computation.3 | async-start | bytes 1835008 | tf_op jit(solution)/shard_map/all_to_all | solution.py:55
  333.4 15.6 %all-to-all-done.2 = bf16[32,2,7168]{2,1,0:T(2,128)(2,1)S(1)} async-done(((bf16[32,2,7168]{2,1,0:T(2,128)(2,1)}), bf16[32,2,7168]{2,1,0:T(2,128)(2,1)S(1)}, u32[]{:S(2)}, u32[]{:S(2)}) %all-to-all-start.2) | async-done | bytes 917536 | tf_op jit(solution)/shard_map/all_to_all | solution.py:55
  349.0 0.3 reshape.90
  349.3 0.0 copy-start.2
  349.3 0.9 gather_fusion
  350.1 0.0 copy-done.2
  350.1 1.0 fusion.11
  (7 shorter events, 0.0 us)
Async XLA Ops:
  6.5 2.0 copy-start
  6.5 316.2 %reduce-scatter.2.cloned.1.call-start = ((), (), s32[]{:S(2)}) async-start(), calls=%async_computation.4 | async-start | bytes 8257536 | tf_op jit(solution)/shard_map/reduce_scatter | solution.py:52
  226.8 6.3 %copy-start.1 = (bf16[512,7168]{1,0:T(8,128)(2,1)S(1)}, bf16[512,7168]{1,0:T(8,128)(2,1)}, u32[]{:S(2)}) copy-start(bf16[512,7168]{1,0:T(8,128)(2,1)} %reshape.85) | copy-start | bytes 22020100
  226.8 7.3 %copy-start.3 = (bf16[1,7168,256]{2,1,0:T(8,128)(2,1)S(1)}, bf16[1,7168,256]{2,1,0:T(8,128)(2,1)}, u32[]{:S(2)}) copy-start(bf16[1,7168,256]{2,1,0:T(8,128)(2,1)} %param.10) | copy-start | bytes 11010052
  325.7 23.2 %all-to-all-start.2 = ((bf16[32,2,7168]{2,1,0:T(2,128)(2,1)}), bf16[32,2,7168]{2,1,0:T(2,128)(2,1)S(1)}, u32[]{:S(2)}, u32[]{:S(2)}) async-start(bf16[32,2,7168]{2,1,0:T(2,128)(2,1)} %copy.11), calls=%async_computation.3 | async-start | bytes 1835008 | tf_op jit(solution)/shard_map/all_to_all | solution.py:55
  349.3 0.9 copy-start.2
Sparse Core Ops, SparseCore 0:
  243.4 79.2 reduce-scatter.1
